TPU v7x, 32 devices: a whole 2x2x4 slice. The times are simulated.
32 devices in a mesh: grp: 8 (over y, x, core), tile: 4 (over z).
Axes of the slice: x: 2, y: 2, z: 4, core: 2. Of those that a mesh axis runs over, the one named last changes fastest.
Arguments:
- atm_flux: float32 [6, 32768], P(None, ('grp', 'tile')), may hold values from -6 to 6
- send_block: int32 [32, 4, 4], P(('grp', 'tile')), may hold values from 0 to 7
- send_count: int32 [32, 4], P(('grp', 'tile')), may hold values from 1 to 4, as said below
- recv_block: int32 [32, 4, 4], P(('grp', 'tile')), may hold values from 0 to 63
- recv_weight: bfloat16 [32, 4, 4, 128, 128], P(('grp', 'tile')), may hold values from -0.5 to 0.5
- sea_temp: float32 [256, 1024], P('grp', 'tile'), may hold values from -6 to 6
- ocean_mask: int32 [256, 1024], P('grp', 'tile'), may hold values 0 or 1
Outputs:
- heat_flux: float32 [256, 1024], P('grp', 'tile')
- stress_curl: float32 [256, 1024], P('grp', 'tile')
- atm_return: float32 [4, 32768], P(None, ('grp', 'tile'))
Inputs may be any that keep to these rules, and one draw needn't show every extreme that they name: `send_count`: in every draw a quarter of the tile indices, drawn from the seed, receive exactly 4 blocks from every device of their group; every other pair carries 1 to 2 blocks.
All inputs are finite; a program needn't handle non-finite values. No bound on the sum of `ocean_mask` on one device may be relied on, other than what follows from the above.
Results may differ from a plain program's by a relative error of at most 0.0003.
Values sent between devices are 32-bit elements; how exact they have to be, the bound alone decides.
A program may use at most 64 MiB of HBM per device.

v0:
```python
import jax
import jax.numpy as jnp
from jax import lax
from jax.sharding import PartitionSpec as P

precise = lax.Precision.HIGHEST


def extended(block, sides, width):
    for axis, dim in sides:
        count = lax.axis_size(axis)
        forward = [(i, i + 1) for i in range(count - 1)]
        forward.append((count - 1, 0))
        backward = [(target, source) for source, target in forward]
        low = lax.ppermute(
            lax.slice_in_dim(block, block.shape[dim] - width, None, axis=dim), axis, forward
        )
        high = lax.ppermute(lax.slice_in_dim(block, 0, width, axis=dim), axis, backward)
        block = jnp.concatenate([low, block, high], axis=dim)
    return block


def from_partner(value, axis, stride):
    return lax.ppermute(value, axis, [(i, i ^ 1 << stride) for i in range(lax.axis_size(axis))])


def bulk_formula(fields, surface_temp, ocean_mask):
    sea_share = ocean_mask.astype(jnp.float32)
    wind_u, wind_v, air_temp, air_vapor, short_down, long_down = [fields[k] for k in range(6)]
    wind_speed = jnp.sqrt(wind_u * wind_u + wind_v * wind_v + 0.5)
    stress_x = 0.8 * wind_speed * wind_u * sea_share
    stress_y = 0.8 * wind_speed * wind_v * sea_share
    sensible = 0.6 * wind_speed * (surface_temp - air_temp)
    latent = 0.7 * wind_speed * (jnp.exp(0.3 * surface_temp) - air_vapor)
    long_up = 0.4 * (1.0 + 0.2 * surface_temp) ** 4
    heat_flux = (0.94 * short_down + long_down - long_up - sensible - latent) * sea_share
    surface = jnp.stack([surface_temp, sensible, latent, long_up]) * sea_share[None]
    return (stress_x, stress_y, heat_flux, surface)


def per_device(atm_flux, send_block, send_count, recv_block, recv_weight, sea_temp, ocean_mask):
    tile_count = lax.axis_size("tile")
    field_count = atm_flux.shape[0]
    block_cells = recv_weight.shape[-1]
    slot_count = send_block.shape[2]
    atm_blocks = atm_flux.shape[1] // block_cells
    ocean_rows, ocean_cols = sea_temp.shape
    ocean_blocks = ocean_rows * ocean_cols // block_cells
    slot_range = jnp.arange(slot_count, dtype=jnp.int32)
    blocks = atm_flux.reshape(field_count, atm_blocks, block_cells)
    send_index = send_block[0]
    pair_count = send_count[0]
    live_slots = (slot_range[None, :] < pair_count[:, None]).astype(jnp.float32)
    chosen = jnp.take(blocks, send_index, axis=1) * live_slots[None, :, :, None]
    incoming = lax.all_to_all(chosen, "tile", split_axis=1, concat_axis=1, tiled=True)
    weight_wide = recv_weight[0].astype(jnp.float32)
    remapped = jnp.einsum("scij,fscj->fsci", weight_wide, incoming, precision=precise)
    dest_block = recv_block[0]
    onehot = (
        jnp.arange(ocean_blocks, dtype=jnp.int32)[:, None] == dest_block.reshape(-1)[None, :]
    ).astype(jnp.float32)
    landed = jnp.einsum(
        "ok,fkj->foj",
        onehot,
        remapped.reshape(field_count, tile_count * slot_count, block_cells),
        precision=precise,
    )
    fields = landed.reshape(field_count, ocean_rows, ocean_cols)
    stress_x, stress_y, heat_flux, surface = bulk_formula(fields, sea_temp, ocean_mask)
    sea_share = ocean_mask.astype(jnp.float32)
    padded = extended(jnp.stack([stress_x, stress_y]), (("grp", 1), ("tile", 2)), 1)
    mirror_row = stress_x[ocean_rows - 1]
    for bit_number in range(tile_count.bit_length() - 1):
        mirror_row = from_partner(mirror_row, "tile", bit_number)
    fold_values = -jnp.flip(mirror_row)
    group_index = lax.axis_index("grp")
    south_rim = jnp.where(group_index == 0, 0.0, padded[0, 0, 1:-1])
    north_rim = jnp.where(group_index == lax.axis_size("grp") - 1, fold_values, padded[0, -1, 1:-1])
    column_x = jnp.concatenate([south_rim[None], stress_x, north_rim[None]], axis=0)
    stress_curl = 0.5 * (padded[1, 1:-1, 2:] - padded[1, 1:-1, :-2]) - 0.5 * (
        column_x[2:] - column_x[:-2]
    )
    stress_curl = stress_curl * sea_share
    surface_blocks = surface.reshape(surface.shape[0], ocean_blocks, block_cells)
    chosen_back = jnp.take(surface_blocks, dest_block, axis=1)
    returned = jnp.einsum("scij,fsci->fscj", weight_wide, chosen_back, precision=precise)
    arrived = lax.all_to_all(returned, "tile", split_axis=1, concat_axis=1, tiled=True)
    arrived = arrived * live_slots[None, :, :, None]
    atm_onehot = (
        jnp.arange(atm_blocks, dtype=jnp.int32)[:, None] == send_index.reshape(-1)[None, :]
    ).astype(jnp.float32)
    atm_part = jnp.einsum(
        "ak,fkj->faj",
        atm_onehot,
        arrived.reshape(surface.shape[0], tile_count * slot_count, block_cells),
        precision=precise,
    )
    return (heat_flux, stress_curl, atm_part.reshape(surface.shape[0], atm_blocks * block_cells))


def solution(mesh):
    placed = (
        P(None, ("grp", "tile")),
        P(("grp", "tile"), None, None),
        P(("grp", "tile"), None),
        P(("grp", "tile"), None, None),
        P(("grp", "tile"), None, None, None, None),
        P("grp", "tile"),
        P("grp", "tile"),
    )
    return jax.shard_map(
        per_device,
        mesh=mesh,
        in_specs=placed,
        out_specs=(P("grp", "tile"), P("grp", "tile"), P(None, ("grp", "tile"))),
        check_vma=False,
    )
```

profile of v0, /device:TPU:0, one launch (start us, length us, event | category | flops | bytes accessed | tf_op | source)
XLA Modules:
  0.0 37.9 jit_solution(13872398486308174749)
XLA Ops:
  0.6 0.7 %compare_select_fusion.2 = s32[4,4,1]{1,0,2:T(4,128)S(1)} fusion(s32[1,4,4]{2,1,0:T(4,128)} %param.8), kind=kLoop, calls=%fused_computation.52 | loop fusion | flops 48 | bytes 128 | tf_op jit(solution)/shard_map/jit(_take)/jit(_where)/select_n | solution.py:54
  1.5 0.7 %copy-done.4 = s32[1,4,4]{2,1,0:T(4,128)S(1)} copy-done((s32[1,4,4]{2,1,0:T(4,128)S(1)}, s32[1,4,4]{2,1,0:T(4,128)}, u32[]{:S(2)}) %copy-start.4) | copy-done | bytes 88
  2.2 1.3 %gather_fusion = f32[16,6,128]{2,1,0:T(8,128)S(1)} fusion(f32[6,8,128]{2,0,1:T(8,128)} %bitcast.69, s32[1024]{0:T(1024)S(1)} %pad_clamp_fusion.1), kind=kCustom, calls=%fused_computation | custom fusion | bytes 98368 | tf_op jit(solution)/shard_map/jit(_take)/gather | solution.py:54
  3.6 0.7 %fusion.6 = f32[6,4,4,128]{3,2,0,1:T(4,128)} fusion(f32[4,4,6,128]{3,2,1,0:T(8,128)S(1)} %bitcast.65, f32[4,4]{1,0:T(4,128)S(1)} %get-tuple-element.21, pred[4,4]{1,0:T(4,128)(4,1)S(1)} %get-tuple-element.22), kind=kLoop, calls=%fused_computation.14 | loop fusion | flops 24576 | bytes 98384 | tf_op jit(solution)/shard_map/mul | solution.py:54
  4.3 6.5 %all-to-all-start = ((f32[6,4,4,128]{3,2,0,1:T(4,128)}), f32[6,4,4,128]{3,2,0,1:T(4,128)S(1)}, u32[]{:S(2)}, u32[]{:S(2)}) async-start(f32[6,4,4,128]{3,2,0,1:T(4,128)} %fusion.6), calls=%async_computation | async-start | bytes 98304 | tf_op jit(solution)/shard_map/all_to_all | solution.py:55
  11.0 0.7 %copy-done.1 = s32[32,256]{1,0:T(8,128)S(1)} copy-done((s32[32,256]{1,0:T(8,128)S(1)}, s32[32,256]{1,0:T(8,128)}, u32[]{:S(2)}) %copy-start.1) | copy-done | bytes 32792
  11.8 4.7 %all-to-all-done = f32[6,4,4,128]{3,2,0,1:T(4,128)S(1)} async-done(((f32[6,4,4,128]{3,2,0,1:T(4,128)}), f32[6,4,4,128]{3,2,0,1:T(4,128)S(1)}, u32[]{:S(2)}, u32[]{:S(2)}) %all-to-all-start) | async-done | bytes 49184 | tf_op jit(solution)/shard_map/all_to_all | solution.py:55
  16.4 0.9 %fusion.1 = f32[4,4,6,128]{3,2,1,0:T(8,128)S(1)} fusion(bf16[1,4,4,128,128]{4,3,2,1,0:T(8,128)(2,1)S(1)} %copy-done, f32[6,4,4,128]{3,2,0,1:T(4,128)S(1)} %all-to-all-done), kind=kOutput, calls=%fused_computation.6 | convolution fusion | flops 18874368 | bytes 622592 | tf_op jit(solution)/shard_map/scij,fscj->fsci/dot_general | solution.py:57
  17.4 0.4 convolution_bitcast_fusion
  17.8 0.7 %multiply_bitcast_fusion = (f32[1,32,256]{2,1,0:T(8,128)S(1)}, f32[32,256]{1,0:T(8,128)S(1)}, f32[32,256]{1,0:T(8,128)}, f32[32,256]{1,0:T(8,128)S(1)}, f32[32,256]{1,0:T(8,128)S(1)}, /*index=5*/f32[32,256]{1,0:T(8,128)S(1)}) fusion(f32[32,256]{1,0:T(8,128)S(1)} %squeeze.40, s32[32,256]{1,0:T(8,128)S(1)} %copy-done.1, f32[32,256]{1,0:T(8,128)S(1)} %squeeze.39, ...), kind=kLoop, calls=%fused_computation.37 | loop fusion | flops 212992 | bytes 425984 | tf_op jit(solution)/shard_map/stack | solution.py:71
  18.6 2.6 %collective-permute-start.1 = (f32[2,1,256]{2,1,0:T(1,128)S(1)}, f32[2,1,256]{2,1,0:T(1,128)S(1)}, u32[]{:S(2)}, u32[]{:S(2)}) collective-permute-start(f32[2,1,256]{2,1,0:T(1,128)S(1)} %get-tuple-element.18), channel_id=1, source_target_pairs={{4,0},{8,4},{12,8},{16,12},{20,16},{24,20},{28,24},{0,28},{5,1},{9... | collective-permute-start | bytes 6152 | tf_op jit(solution)/shard_map/ppermute | solution.py:18
  21.2 0.8 %collective-permute-start.4 = (f32[256]{0:T(256)S(1)}, f32[256]{0:T(256)S(1)}, u32[]{:S(2)}, u32[]{:S(2)}) collective-permute-start(f32[256]{0:T(256)S(1)} %bitcast.73), channel_id=1, source_target_pairs={{0,1},{1,0},{2,3},{3,2},{4,5},{5,4},{6,7},{7,6},{8,9},{9,8},{10,11... | collective-permute-start | bytes 3080 | tf_op jit(solution)/shard_map/ppermute | solution.py:24
  22.2 0.1 maximum_multiply_fusion
  22.3 0.6 %gather_fusion.1 = f32[16,4,128]{2,1,0:T(4,128)S(1)} fusion(f32[4,64,128]{2,0,1:T(4,128)S(1)} %maximum_multiply_fusion, s32[1024]{0:T(1024)S(1)} %pad_clamp_fusion), kind=kCustom, calls=%fused_computation.1 | custom fusion | bytes 65600 | tf_op jit(solution)/shard_map/jit(_take)/gather | solution.py:85
  22.9 1.2 %convolution_bitcast_fusion.1 = f32[4,4,4,128]{3,0,2,1:T(4,128)} fusion(bf16[1,4,4,128,128]{4,3,2,1,0:T(8,128)(2,1)S(1)} %copy-done, f32[4,4,4,128]{3,2,1,0:T(4,128)S(1)} %bitcast.68, pred[4,4]{1,0:T(4,128)(4,1)S(1)} %compare_and_fusion), kind=kOutput, calls=%fused_computation.3 | convolution fusion | flops 12591104 | bytes 589840 | tf_op jit(solution)/shard_map/scij,fsci->fscj/dot_general | solution.py:86
  24.1 3.3 %all-to-all-start.1 = ((f32[4,4,4,128]{3,0,2,1:T(4,128)}), f32[4,4,4,128]{3,0,2,1:T(4,128)S(1)}, u32[]{:S(2)}, u32[]{:S(2)}) async-start(f32[4,4,4,128]{3,0,2,1:T(4,128)} %convolution_bitcast_fusion.1), calls=%async_computation.1 | async-start | bytes 65536 | tf_op jit(solution)/shard_map/all_to_all | solution.py:87
  27.4 2.9 %collective-permute-start.5 = (f32[256]{0:T(256)S(1)}, f32[256]{0:T(256)S(1)}, u32[]{:S(2)}, u32[]{:S(2)}) collective-permute-start(f32[256]{0:T(256)S(1)} %collective-permute-done.4), channel_id=1, source_target_pairs={{0,2},{1,3},{2,0},{3,1},{4,6},{5,7},{6,4},{7,5},{8,10},{9,11},{10,... | collective-permute-start | bytes 3080 | tf_op jit(solution)/shard_map/ppermute | solution.py:24
  30.4 1.5 %collective-permute-start.3 = (f32[2,34,1]{2,1,0:T(8,128)S(1)}, f32[2,34,1]{2,1,0:T(8,128)S(1)}, u32[]{:S(2)}, u32[]{:S(2)}) collective-permute-start(f32[2,34,1]{2,1,0:T(8,128)S(1)} %get-tuple-element.17), channel_id=1, source_target_pairs={{0,1},{1,2},{2,3},{3,0},{4,5},{5,6},{6,7},{7,4},{8,9},{9,10},{10,1... | collective-permute-start | bytes 824 | tf_op jit(solution)/shard_map/ppermute | solution.py:15
  31.9 2.4 %collective-permute-start.2 = (f32[2,34,1]{2,1,0:T(8,128)S(1)}, f32[2,34,1]{2,1,0:T(8,128)S(1)}, u32[]{:S(2)}, u32[]{:S(2)}) collective-permute-start(f32[2,34,1]{2,1,0:T(8,128)S(1)} %get-tuple-element.16), channel_id=1, source_target_pairs={{1,0},{2,1},{3,2},{0,3},{5,4},{6,5},{7,6},{4,7},{9,8},{10,9},{11,1... | collective-permute-start | bytes 824 | tf_op jit(solution)/shard_map/ppermute | solution.py:18
  34.3 0.7 %slice-done = f32[1,1,256]{2,1,0:T(1,128)S(1)} async-done(((f32[2,1,256]{2,1,0:T(1,128)}), f32[1,1,256]{2,1,0:T(1,128)S(1)}, s32[]{:S(2)}) %slice-start) | async-done | bytes 1048 | tf_op jit(solution)/shard_map/slice | solution.py:78
  35.0 1.3 %collective-permute-done.3 = f32[2,34,1]{2,1,0:T(8,128)S(1)} collective-permute-done((f32[2,34,1]{2,1,0:T(8,128)S(1)}, f32[2,34,1]{2,1,0:T(8,128)S(1)}, u32[]{:S(2)}, u32[]{:S(2)}) %collective-permute-start.3) | collective-permute-done | bytes 304 | tf_op jit(solution)/shard_map/ppermute | solution.py:15
  36.3 0.7 %fusion.10 = f32[32,256]{1,0:T(8,128)} fusion(f32[32,256]{1,0:T(8,128)S(1)} %get-tuple-element.12, f32[1,256]{1,0:T(1,128)S(1)} %fusion.26, f32[1,256]{1,0:T(1,128)S(1)} %bitcast.72, f32[2,34,1]{2,1,0:T(8,128)S(1)} %collective-permute-done.3, f32[2,1,256]{2,1,0:T(1,128)S(1)} %copy-done.6, f32[2,1,256]{2,1,0:T(1,128)S(1)} %collective-permute-done, ...), kind=kLoop, calls=%fused_computation.19 | loop fusion | flops 139264 | bytes 170528 | tf_op jit(solution)/shard_map/mul | solution.py:83
  37.1 0.1 convolution_bitcast_fusion.2
  37.2 0.6 %copy.32 = f32[1,4,8,128]{3,1,2,0:T(4,128)} copy(f32[1,4,8,128]{3,2,1,0:T(8,128)S(1)} %convolution_bitcast_fusion.2) | data formatting | bytes 32768
  (51 shorter events, 1.0 us)
Async XLA Ops:
  0.6 15.8 %copy-start = (bf16[1,4,4,128,128]{4,3,2,1,0:T(8,128)(2,1)S(1)}, bf16[1,4,4,128,128]{4,3,2,1,0:T(8,128)(2,1)}, u32[]{:S(2)}) copy-start(bf16[1,4,4,128,128]{4,3,2,1,0:T(8,128)(2,1)} %param.11) | copy-start | bytes 1572868
  1.5 0.7 %copy-start.4 = (s32[1,4,4]{2,1,0:T(4,128)S(1)}, s32[1,4,4]{2,1,0:T(4,128)}, u32[]{:S(2)}) copy-start(s32[1,4,4]{2,1,0:T(4,128)} %param.8) | copy-start | bytes 196
  1.5 0.7 %copy-start.7 = (s32[1,4]{1,0:T(1,128)S(1)}, s32[1,4]{1,0:T(1,128)}, u32[]{:S(2)}) copy-start(s32[1,4]{1,0:T(1,128)} %param.9) | copy-start | bytes 52
  4.3 6.5 %copy-start.3 = (s32[1,4,4]{2,1,0:T(4,128)S(1)}, s32[1,4,4]{2,1,0:T(4,128)}, u32[]{:S(2)}) copy-start(s32[1,4,4]{2,1,0:T(4,128)} %param.10) | copy-start | bytes 196
  4.3 6.7 %copy-start.2 = (f32[32,256]{1,0:T(8,128)S(1)}, f32[32,256]{1,0:T(8,128)}, u32[]{:S(2)}) copy-start(f32[32,256]{1,0:T(8,128)} %param.12) | copy-start | bytes 98308
  4.3 12.2 %all-to-all-start = ((f32[6,4,4,128]{3,2,0,1:T(4,128)}), f32[6,4,4,128]{3,2,0,1:T(4,128)S(1)}, u32[]{:S(2)}, u32[]{:S(2)}) async-start(f32[6,4,4,128]{3,2,0,1:T(4,128)} %fusion.6), calls=%async_computation | async-start | bytes 98304 | tf_op jit(solution)/shard_map/all_to_all | solution.py:55
  10.9 0.8 %copy-start.1 = (s32[32,256]{1,0:T(8,128)S(1)}, s32[32,256]{1,0:T(8,128)}, u32[]{:S(2)}) copy-start(s32[32,256]{1,0:T(8,128)} %param.13) | copy-start | bytes 98308
  18.5 11.7 %collective-permute-start = (f32[2,1,256]{2,1,0:T(1,128)S(1)}, f32[2,1,256]{2,1,0:T(1,128)S(1)}, u32[]{:S(2)}, u32[]{:S(2)}) collective-permute-start(f32[2,1,256]{2,1,0:T(1,128)S(1)} %get-tuple-element.19), channel_id=1, source_target_pairs={{0,4},{4,8},{8,12},{12,16},{16,20},{20,24},{24,28},{28,0},{1,5},{5... | collective-permute-start | bytes 6152 | tf_op jit(solution)/shard_map/ppermute | solution.py:15
  18.6 11.7 %collective-permute-start.1 = (f32[2,1,256]{2,1,0:T(1,128)S(1)}, f32[2,1,256]{2,1,0:T(1,128)S(1)}, u32[]{:S(2)}, u32[]{:S(2)}) collective-permute-start(f32[2,1,256]{2,1,0:T(1,128)S(1)} %get-tuple-element.18), channel_id=1, source_target_pairs={{4,0},{8,4},{12,8},{16,12},{20,16},{24,20},{28,24},{0,28},{5,1},{9... | collective-permute-start | bytes 6152 | tf_op jit(solution)/shard_map/ppermute | solution.py:18
  21.2 6.2 %collective-permute-start.4 = (f32[256]{0:T(256)S(1)}, f32[256]{0:T(256)S(1)}, u32[]{:S(2)}, u32[]{:S(2)}) collective-permute-start(f32[256]{0:T(256)S(1)} %bitcast.73), channel_id=1, source_target_pairs={{0,1},{1,0},{2,3},{3,2},{4,5},{5,4},{6,7},{7,6},{8,9},{9,8},{10,11... | collective-permute-start | bytes 3080 | tf_op jit(solution)/shard_map/ppermute | solution.py:24
  24.1 12.9 %all-to-all-start.1 = ((f32[4,4,4,128]{3,0,2,1:T(4,128)}), f32[4,4,4,128]{3,0,2,1:T(4,128)S(1)}, u32[]{:S(2)}, u32[]{:S(2)}) async-start(f32[4,4,4,128]{3,0,2,1:T(4,128)} %convolution_bitcast_fusion.1), calls=%async_computation.1 | async-start | bytes 65536 | tf_op jit(solution)/shard_map/all_to_all | solution.py:87
  27.4 6.8 %collective-permute-start.5 = (f32[256]{0:T(256)S(1)}, f32[256]{0:T(256)S(1)}, u32[]{:S(2)}, u32[]{:S(2)}) collective-permute-start(f32[256]{0:T(256)S(1)} %collective-permute-done.4), channel_id=1, source_target_pairs={{0,2},{1,3},{2,0},{3,1},{4,6},{5,7},{6,4},{7,5},{8,10},{9,11},{10,... | collective-permute-start | bytes 3080 | tf_op jit(solution)/shard_map/ppermute | solution.py:24
  30.3 3.9 %copy-start.5 = (f32[2,1,256]{2,1,0:T(1,128)}, f32[2,1,256]{2,1,0:T(1,128)S(1)}, u32[]{:S(2)}) copy-start(f32[2,1,256]{2,1,0:T(1,128)S(1)} %collective-permute-done.1) | copy-start | bytes 6148
  30.4 5.9 %collective-permute-start.3 = (f32[2,34,1]{2,1,0:T(8,128)S(1)}, f32[2,34,1]{2,1,0:T(8,128)S(1)}, u32[]{:S(2)}, u32[]{:S(2)}) collective-permute-start(f32[2,34,1]{2,1,0:T(8,128)S(1)} %get-tuple-element.17), channel_id=1, source_target_pairs={{0,1},{1,2},{2,3},{3,0},{4,5},{5,6},{6,7},{7,4},{8,9},{9,10},{10,1... | collective-permute-start | bytes 824 | tf_op jit(solution)/shard_map/ppermute | solution.py:15
  31.9 4.4 %collective-permute-start.2 = (f32[2,34,1]{2,1,0:T(8,128)S(1)}, f32[2,34,1]{2,1,0:T(8,128)S(1)}, u32[]{:S(2)}, u32[]{:S(2)}) collective-permute-start(f32[2,34,1]{2,1,0:T(8,128)S(1)} %get-tuple-element.16), channel_id=1, source_target_pairs={{1,0},{2,1},{3,2},{0,3},{5,4},{6,5},{7,6},{4,7},{9,8},{10,9},{11,1... | collective-permute-start | bytes 824 | tf_op jit(solution)/shard_map/ppermute | solution.py:18
  34.3 0.7 %slice-start = ((f32[2,1,256]{2,1,0:T(1,128)}), f32[1,1,256]{2,1,0:T(1,128)S(1)}, s32[]{:S(2)}) async-start(f32[2,1,256]{2,1,0:T(1,128)} %copy-done.5), calls=%async_computation.2 | async-start | bytes 2048 | tf_op jit(solution)/shard_map/slice | solution.py:78
  35.0 1.3 %copy-start.6 = (f32[2,1,256]{2,1,0:T(1,128)S(1)}, f32[2,1,256]{2,1,0:T(1,128)}, u32[]{:S(2)}) copy-start(f32[2,1,256]{2,1,0:T(1,128)} %copy-done.5) | copy-start | bytes 6148
where the time goes:
time: 38.4 us; the launch traced here: 37.9 us
  starting transfers between devices  20 us (52%)
  waiting for transfers between devices  5.95 us (15%)
  local copies, waits for them, and re-layouts  5.32 us (14%)
  other arithmetic  3.19 us (8%)
  matrix products  2.61 us (7%)
  between operations  0.82 us (2%)
    all_to_all x1, starting transfers between devices, per_device(): lax.all_to_all(chosen, 'tile', split_axis=1, concat_axis=1, tiled=True)  6.48 us
    ppermute x2, starting transfers between devices, extended(): lax.ppermute(lax.slice_in_dim(block, 0, width, axis=dim), axis, backward)  4.99 us
    all_to_all x1, waiting for transfers between devices, per_device(): lax.all_to_all(chosen, 'tile', split_axis=1, concat_axis=1, tiled=True)  4.65 us
    ppermute x2, starting transfers between devices, from_partner(): lax.ppermute(value, axis, [(i, i ^ 1 << stride) for i in range(lax.axis_s...  3.71 us
    all_to_all x1, starting transfers between devices, per_device(): lax.all_to_all(returned, 'tile', split_axis=1, concat_axis=1, tiled=True)  3.26 us
    unnamed x17, local copies, waits for them, and re-layouts  2.03 us
    ppermute x2, starting transfers between devices, extended(): lax.ppermute(lax.slice_in_dim(block, block.shape[dim] - width, None, axis...  1.53 us
    gather x1, local copies, waits for them, and re-layouts, per_device(): chosen = jnp.take(blocks, send_index, axis=1) * live_slots[None, :, :, None]  1.31 us
  transfers between devices with their start and end apart: 8, of which 2 were waited for; matrix products, arithmetic and copies ran while one was open for 9% of the time, Pallas kernels for 0%

commit v1 on v0

--- a/solution.py
+++ b/solution.py
@@ -84,7 +84,10 @@
     surface_blocks = surface.reshape(surface.shape[0], ocean_blocks, block_cells)
     chosen_back = jnp.take(surface_blocks, dest_block, axis=1)
     returned = jnp.einsum("scij,fsci->fscj", weight_wide, chosen_back, precision=precise)
-    arrived = lax.all_to_all(returned, "tile", split_axis=1, concat_axis=1, tiled=True)
+    arrived = jnp.concatenate(
+        lax.all_to_all(jnp.stack(jnp.split(returned, lax.axis_size("tile"), axis=1)), "tile", 0, 0),
+        axis=1,
+    )
     arrived = arrived * live_slots[None, :, :, None]
     atm_onehot = (
         jnp.arange(atm_blocks, dtype=jnp.int32)[:, None] == send_index.reshape(-1)[None, :]

time: 38.4 us -> 38.3 us (level)
  matrix products: 2.61 us -> 2.05 us
  other arithmetic: 3.19 us -> 3.73 us
    dot_general x1, matrix products: 1.2 us -> 0.57 us  [per_device(): jnp.einsum('scij,fsci->fscj', weight_wide, chosen_back, precision=precise)]
    another operation x0 -> x1, other arithmetic: none -> 0.62 us  [per_device(): jnp.stack(jnp.split(returned, lax.axis_size('tile'), axis=1))]
where the time goes in v1:
time: 38.3 us; the launch traced here: 37.8 us
  starting transfers between devices  20 us (52%)
  waiting for transfers between devices  5.87 us (15%)
  local copies, waits for them, and re-layouts  5.4 us (14%)
  other arithmetic  3.73 us (10%)
  matrix products  2.05 us (5%)
  between operations  0.81 us (2%)
    all_to_all x1, starting transfers between devices, per_device(): lax.all_to_all(chosen, 'tile', split_axis=1, concat_axis=1, tiled=True)  6.48 us
    ppermute x2, starting transfers between devices, extended(): lax.ppermute(lax.slice_in_dim(block, 0, width, axis=dim), axis, backward)  4.99 us
    all_to_all x1, waiting for transfers between devices, per_device(): lax.all_to_all(chosen, 'tile', split_axis=1, concat_axis=1, tiled=True)  4.57 us
    ppermute x2, starting transfers between devices, from_partner(): lax.ppermute(value, axis, [(i, i ^ 1 << stride) for i in range(lax.axis_s...  3.71 us
    all_to_all x1, starting transfers between devices, per_device(): lax.all_to_all(jnp.stack(jnp.split(returned, lax.axis_size('tile'), axis=...  3.26 us
    unnamed x17, local copies, waits for them, and re-layouts  2.03 us
    ppermute x2, starting transfers between devices, extended(): lax.ppermute(lax.slice_in_dim(block, block.shape[dim] - width, None, axis...  1.53 us
    gather x1, local copies, waits for them, and re-layouts, per_device(): chosen = jnp.take(blocks, send_index, axis=1) * live_slots[None, :, :, None]  1.31 us
  transfers between devices with their start and end apart: 8, of which 2 were waited for; matrix products, arithmetic and copies ran while one was open for 9% of the time, Pallas kernels for 0%

profile of v1, /device:TPU:0, one launch (start us, length us, event | category | flops | bytes accessed | tf_op | source)
XLA Modules:
  0.0 37.8 jit_solution(5915072367134180304)
XLA Ops:
  0.6 0.7 %compare_select_fusion.2 = s32[4,4,1]{1,0,2:T(4,128)S(1)} fusion(s32[1,4,4]{2,1,0:T(4,128)} %param.8), kind=kLoop, calls=%fused_computation.57 | loop fusion | flops 48 | bytes 128 | tf_op jit(solution)/shard_map/jit(_take)/jit(_where)/select_n | solution.py:54
  1.5 0.7 %copy-done.4 = s32[1,4,4]{2,1,0:T(4,128)S(1)} copy-done((s32[1,4,4]{2,1,0:T(4,128)S(1)}, s32[1,4,4]{2,1,0:T(4,128)}, u32[]{:S(2)}) %copy-start.4) | copy-done | bytes 88
  2.2 1.3 %gather_fusion = f32[16,6,128]{2,1,0:T(8,128)S(1)} fusion(f32[6,8,128]{2,0,1:T(8,128)} %bitcast.78, s32[1024]{0:T(1024)S(1)} %pad_clamp_fusion.1), kind=kCustom, calls=%fused_computation | custom fusion | bytes 98368 | tf_op jit(solution)/shard_map/jit(_take)/gather | solution.py:54
  3.6 0.7 %fusion.6 = f32[6,4,4,128]{3,2,0,1:T(4,128)} fusion(f32[4,4,6,128]{3,2,1,0:T(8,128)S(1)} %bitcast.75, f32[4,4]{1,0:T(4,128)S(1)} %get-tuple-element.25, pred[4,4]{1,0:T(4,128)(4,1)S(1)} %get-tuple-element.26), kind=kLoop, calls=%fused_computation.14 | loop fusion | flops 24576 | bytes 98384 | tf_op jit(solution)/shard_map/mul | solution.py:54
  4.3 6.5 %all-to-all-start = ((f32[6,4,4,128]{3,2,0,1:T(4,128)}), f32[6,4,4,128]{3,2,0,1:T(4,128)S(1)}, u32[]{:S(2)}, u32[]{:S(2)}) async-start(f32[6,4,4,128]{3,2,0,1:T(4,128)} %fusion.6), calls=%async_computation | async-start | bytes 98304 | tf_op jit(solution)/shard_map/all_to_all | solution.py:55
  11.0 0.7 %copy-done.1 = s32[32,256]{1,0:T(8,128)S(1)} copy-done((s32[32,256]{1,0:T(8,128)S(1)}, s32[32,256]{1,0:T(8,128)}, u32[]{:S(2)}) %copy-start.1) | copy-done | bytes 32792
  11.9 4.6 %all-to-all-done = f32[6,4,4,128]{3,2,0,1:T(4,128)S(1)} async-done(((f32[6,4,4,128]{3,2,0,1:T(4,128)}), f32[6,4,4,128]{3,2,0,1:T(4,128)S(1)}, u32[]{:S(2)}, u32[]{:S(2)}) %all-to-all-start) | async-done | bytes 49184 | tf_op jit(solution)/shard_map/all_to_all | solution.py:55
  16.4 0.9 %fusion.1 = f32[4,4,6,128]{3,2,1,0:T(8,128)S(1)} fusion(bf16[1,4,4,128,128]{4,3,2,1,0:T(8,128)(2,1)S(1)} %copy-done, f32[6,4,4,128]{3,2,0,1:T(4,128)S(1)} %all-to-all-done), kind=kOutput, calls=%fused_computation.6 | convolution fusion | flops 18874368 | bytes 622592 | tf_op jit(solution)/shard_map/scij,fscj->fsci/dot_general | solution.py:57
  17.3 0.4 convolution_bitcast_fusion
  17.8 0.7 %multiply_bitcast_fusion = (f32[1,32,256]{2,1,0:T(8,128)S(1)}, f32[32,256]{1,0:T(8,128)S(1)}, f32[32,256]{1,0:T(8,128)}, f32[32,256]{1,0:T(8,128)S(1)}, f32[32,256]{1,0:T(8,128)S(1)}, /*index=5*/f32[32,256]{1,0:T(8,128)S(1)}) fusion(f32[32,256]{1,0:T(8,128)S(1)} %squeeze.40, s32[32,256]{1,0:T(8,128)S(1)} %copy-done.1, f32[32,256]{1,0:T(8,128)S(1)} %squeeze.39, ...), kind=kLoop, calls=%fused_computation.38 | loop fusion | flops 212992 | bytes 425984 | tf_op jit(solution)/shard_map/stack | solution.py:71
  18.6 2.6 %collective-permute-start.1 = (f32[2,1,256]{2,1,0:T(1,128)S(1)}, f32[2,1,256]{2,1,0:T(1,128)S(1)}, u32[]{:S(2)}, u32[]{:S(2)}) collective-permute-start(f32[2,1,256]{2,1,0:T(1,128)S(1)} %get-tuple-element.18), channel_id=1, source_target_pairs={{4,0},{8,4},{12,8},{16,12},{20,16},{24,20},{28,24},{0,28},{5,1},{9... | collective-permute-start | bytes 6152 | tf_op jit(solution)/shard_map/ppermute | solution.py:18
  21.2 0.8 %collective-permute-start.4 = (f32[256]{0:T(256)S(1)}, f32[256]{0:T(256)S(1)}, u32[]{:S(2)}, u32[]{:S(2)}) collective-permute-start(f32[256]{0:T(256)S(1)} %bitcast.83), channel_id=1, source_target_pairs={{0,1},{1,0},{2,3},{3,2},{4,5},{5,4},{6,7},{7,6},{8,9},{9,8},{10,11... | collective-permute-start | bytes 3080 | tf_op jit(solution)/shard_map/ppermute | solution.py:24
  22.3 0.6 %gather_fusion.1 = f32[16,4,128]{2,1,0:T(4,128)S(1)} fusion(f32[4,64,128]{2,0,1:T(4,128)S(1)} %maximum_multiply_fusion, s32[1024]{0:T(1024)S(1)} %pad_clamp_fusion), kind=kCustom, calls=%fused_computation.1 | custom fusion | bytes 65600 | tf_op jit(solution)/shard_map/jit(_take)/gather | solution.py:85
  22.9 0.6 %convolution_bitcast_fusion.1 = f32[4,4,4,128]{3,0,2,1:T(4,128)S(1)} fusion(bf16[1,4,4,128,128]{4,3,2,1,0:T(8,128)(2,1)S(1)} %copy-done, f32[4,4,4,128]{3,2,1,0:T(4,128)S(1)} %bitcast.77, pred[4,4]{1,0:T(4,128)(4,1)S(1)} %compare_and_fusion), kind=kOutput, calls=%fused_computation.3 | convolution fusion | flops 12591104 | bytes 589840 | tf_op jit(solution)/shard_map/scij,fsci->fscj/dot_general | solution.py:86
  23.5 0.6 %pad_maximum_fusion.11 = f32[4,4,1,4,128]{4,1,3,2,0:T(4,128)} fusion(f32[1,4,1,4,128]{4,1,3,2,0:T(4,128)S(1)} %get-tuple-element.22, f32[1,4,1,4,128]{4,1,3,2,0:T(4,128)S(1)} %get-tuple-element.23, f32[1,4,1,4,128]{4,1,3,2,0:T(4,128)S(1)} %get-tuple-element.24, f32[1,4,1,4,128]{4,1,3,2,0:T(4,128)S(1)} %get-tuple-element.21), kind=kLoop, calls=%fused_computation.34 | loop fusion | flops 24576 | bytes 65536 | tf_op jit(solution)/shard_map/stack | solution.py:88
  24.1 3.3 %all-to-all-start.1 = ((f32[4,4,1,4,128]{4,1,3,2,0:T(4,128)}), f32[4,4,1,4,128]{4,1,3,2,0:T(4,128)S(1)}, u32[]{:S(2)}, u32[]{:S(2)}) async-start(f32[4,4,1,4,128]{4,1,3,2,0:T(4,128)} %pad_maximum_fusion.11), calls=%async_computation.1 | async-start | bytes 65536 | tf_op jit(solution)/shard_map/all_to_all | solution.py:88
  27.4 2.9 %collective-permute-start.5 = (f32[256]{0:T(256)S(1)}, f32[256]{0:T(256)S(1)}, u32[]{:S(2)}, u32[]{:S(2)}) collective-permute-start(f32[256]{0:T(256)S(1)} %collective-permute-done.4), channel_id=1, source_target_pairs={{0,2},{1,3},{2,0},{3,1},{4,6},{5,7},{6,4},{7,5},{8,10},{9,11},{10,... | collective-permute-start | bytes 3080 | tf_op jit(solution)/shard_map/ppermute | solution.py:24
  30.4 1.5 %collective-permute-start.3 = (f32[2,34,1]{2,1,0:T(8,128)S(1)}, f32[2,34,1]{2,1,0:T(8,128)S(1)}, u32[]{:S(2)}, u32[]{:S(2)}) collective-permute-start(f32[2,34,1]{2,1,0:T(8,128)S(1)} %get-tuple-element.17), channel_id=1, source_target_pairs={{0,1},{1,2},{2,3},{3,0},{4,5},{5,6},{6,7},{7,4},{8,9},{9,10},{10,1... | collective-permute-start | bytes 824 | tf_op jit(solution)/shard_map/ppermute | solution.py:15
  31.8 2.4 %collective-permute-start.2 = (f32[2,34,1]{2,1,0:T(8,128)S(1)}, f32[2,34,1]{2,1,0:T(8,128)S(1)}, u32[]{:S(2)}, u32[]{:S(2)}) collective-permute-start(f32[2,34,1]{2,1,0:T(8,128)S(1)} %get-tuple-element.16), channel_id=1, source_target_pairs={{1,0},{2,1},{3,2},{0,3},{5,4},{6,5},{7,6},{4,7},{9,8},{10,9},{11,1... | collective-permute-start | bytes 824 | tf_op jit(solution)/shard_map/ppermute | solution.py:18
  34.3 0.7 %slice-done = f32[1,1,256]{2,1,0:T(1,128)S(1)} async-done(((f32[2,1,256]{2,1,0:T(1,128)}), f32[1,1,256]{2,1,0:T(1,128)S(1)}, s32[]{:S(2)}) %slice-start) | async-done | bytes 1048 | tf_op jit(solution)/shard_map/slice | solution.py:78
  35.0 1.3 %collective-permute-done.3 = f32[2,34,1]{2,1,0:T(8,128)S(1)} collective-permute-done((f32[2,34,1]{2,1,0:T(8,128)S(1)}, f32[2,34,1]{2,1,0:T(8,128)S(1)}, u32[]{:S(2)}, u32[]{:S(2)}) %collective-permute-start.3) | collective-permute-done | bytes 304 | tf_op jit(solution)/shard_map/ppermute | solution.py:15
  36.3 0.7 %fusion.10 = f32[32,256]{1,0:T(8,128)} fusion(f32[32,256]{1,0:T(8,128)S(1)} %get-tuple-element.12, f32[1,256]{1,0:T(1,128)S(1)} %fusion.26, f32[1,256]{1,0:T(1,128)S(1)} %bitcast.82, f32[2,34,1]{2,1,0:T(8,128)S(1)} %collective-permute-done.3, f32[2,1,256]{2,1,0:T(1,128)S(1)} %copy-done.6, f32[2,1,256]{2,1,0:T(1,128)S(1)} %collective-permute-done, ...), kind=kLoop, calls=%fused_computation.19 | loop fusion | flops 139264 | bytes 170528 | tf_op jit(solution)/shard_map/mul | solution.py:83
  37.0 0.2 convolution_bitcast_fusion.2
  37.2 0.6 %copy.32 = f32[1,4,8,128]{3,1,2,0:T(4,128)} copy(f32[1,4,8,128]{3,2,1,0:T(8,128)S(1)} %convolution_bitcast_fusion.2) | data formatting | bytes 32768
  (53 shorter events, 1.2 us)
Async XLA Ops:
  0.6 15.8 %copy-start = (bf16[1,4,4,128,128]{4,3,2,1,0:T(8,128)(2,1)S(1)}, bf16[1,4,4,128,128]{4,3,2,1,0:T(8,128)(2,1)}, u32[]{:S(2)}) copy-start(bf16[1,4,4,128,128]{4,3,2,1,0:T(8,128)(2,1)} %param.11) | copy-start | bytes 1572868
  1.5 0.7 %copy-start.4 = (s32[1,4,4]{2,1,0:T(4,128)S(1)}, s32[1,4,4]{2,1,0:T(4,128)}, u32[]{:S(2)}) copy-start(s32[1,4,4]{2,1,0:T(4,128)} %param.8) | copy-start | bytes 196
  1.5 0.7 %copy-start.7 = (s32[1,4]{1,0:T(1,128)S(1)}, s32[1,4]{1,0:T(1,128)}, u32[]{:S(2)}) copy-start(s32[1,4]{1,0:T(1,128)} %param.9) | copy-start | bytes 52
  4.3 6.5 %copy-start.3 = (s32[1,4,4]{2,1,0:T(4,128)S(1)}, s32[1,4,4]{2,1,0:T(4,128)}, u32[]{:S(2)}) copy-start(s32[1,4,4]{2,1,0:T(4,128)} %param.10) | copy-start | bytes 196
  4.3 6.7 %copy-start.2 = (f32[32,256]{1,0:T(8,128)S(1)}, f32[32,256]{1,0:T(8,128)}, u32[]{:S(2)}) copy-start(f32[32,256]{1,0:T(8,128)} %param.12) | copy-start | bytes 98308
  4.3 12.2 %all-to-all-start = ((f32[6,4,4,128]{3,2,0,1:T(4,128)}), f32[6,4,4,128]{3,2,0,1:T(4,128)S(1)}, u32[]{:S(2)}, u32[]{:S(2)}) async-start(f32[6,4,4,128]{3,2,0,1:T(4,128)} %fusion.6), calls=%async_computation | async-start | bytes 98304 | tf_op jit(solution)/shard_map/all_to_all | solution.py:55
  11.0 0.8 %copy-start.1 = (s32[32,256]{1,0:T(8,128)S(1)}, s32[32,256]{1,0:T(8,128)}, u32[]{:S(2)}) copy-start(s32[32,256]{1,0:T(8,128)} %param.13) | copy-start | bytes 98308
  18.5 11.7 %collective-permute-start = (f32[2,1,256]{2,1,0:T(1,128)S(1)}, f32[2,1,256]{2,1,0:T(1,128)S(1)}, u32[]{:S(2)}, u32[]{:S(2)}) collective-permute-start(f32[2,1,256]{2,1,0:T(1,128)S(1)} %get-tuple-element.19), channel_id=1, source_target_pairs={{0,4},{4,8},{8,12},{12,16},{16,20},{20,24},{24,28},{28,0},{1,5},{5... | collective-permute-start | bytes 6152 | tf_op jit(solution)/shard_map/ppermute | solution.py:15
  18.6 11.7 %collective-permute-start.1 = (f32[2,1,256]{2,1,0:T(1,128)S(1)}, f32[2,1,256]{2,1,0:T(1,128)S(1)}, u32[]{:S(2)}, u32[]{:S(2)}) collective-permute-start(f32[2,1,256]{2,1,0:T(1,128)S(1)} %get-tuple-element.18), channel_id=1, source_target_pairs={{4,0},{8,4},{12,8},{16,12},{20,16},{24,20},{28,24},{0,28},{5,1},{9... | collective-permute-start | bytes 6152 | tf_op jit(solution)/shard_map/ppermute | solution.py:18
  21.2 6.2 %collective-permute-start.4 = (f32[256]{0:T(256)S(1)}, f32[256]{0:T(256)S(1)}, u32[]{:S(2)}, u32[]{:S(2)}) collective-permute-start(f32[256]{0:T(256)S(1)} %bitcast.83), channel_id=1, source_target_pairs={{0,1},{1,0},{2,3},{3,2},{4,5},{5,4},{6,7},{7,6},{8,9},{9,8},{10,11... | collective-permute-start | bytes 3080 | tf_op jit(solution)/shard_map/ppermute | solution.py:24
  24.1 12.9 %all-to-all-start.1 = ((f32[4,4,1,4,128]{4,1,3,2,0:T(4,128)}), f32[4,4,1,4,128]{4,1,3,2,0:T(4,128)S(1)}, u32[]{:S(2)}, u32[]{:S(2)}) async-start(f32[4,4,1,4,128]{4,1,3,2,0:T(4,128)} %pad_maximum_fusion.11), calls=%async_computation.1 | async-start | bytes 65536 | tf_op jit(solution)/shard_map/all_to_all | solution.py:88
  27.4 6.8 %collective-permute-start.5 = (f32[256]{0:T(256)S(1)}, f32[256]{0:T(256)S(1)}, u32[]{:S(2)}, u32[]{:S(2)}) collective-permute-start(f32[256]{0:T(256)S(1)} %collective-permute-done.4), channel_id=1, source_target_pairs={{0,2},{1,3},{2,0},{3,1},{4,6},{5,7},{6,4},{7,5},{8,10},{9,11},{10,... | collective-permute-start | bytes 3080 | tf_op jit(solution)/shard_map/ppermute | solution.py:24
  30.3 3.9 %copy-start.5 = (f32[2,1,256]{2,1,0:T(1,128)}, f32[2,1,256]{2,1,0:T(1,128)S(1)}, u32[]{:S(2)}) copy-start(f32[2,1,256]{2,1,0:T(1,128)S(1)} %collective-permute-done.1) | copy-start | bytes 6148
  30.4 5.9 %collective-permute-start.3 = (f32[2,34,1]{2,1,0:T(8,128)S(1)}, f32[2,34,1]{2,1,0:T(8,128)S(1)}, u32[]{:S(2)}, u32[]{:S(2)}) collective-permute-start(f32[2,34,1]{2,1,0:T(8,128)S(1)} %get-tuple-element.17), channel_id=1, source_target_pairs={{0,1},{1,2},{2,3},{3,0},{4,5},{5,6},{6,7},{7,4},{8,9},{9,10},{10,1... | collective-permute-start | bytes 824 | tf_op jit(solution)/shard_map/ppermute | solution.py:15
  31.8 4.4 %collective-permute-start.2 = (f32[2,34,1]{2,1,0:T(8,128)S(1)}, f32[2,34,1]{2,1,0:T(8,128)S(1)}, u32[]{:S(2)}, u32[]{:S(2)}) collective-permute-start(f32[2,34,1]{2,1,0:T(8,128)S(1)} %get-tuple-element.16), channel_id=1, source_target_pairs={{1,0},{2,1},{3,2},{0,3},{5,4},{6,5},{7,6},{4,7},{9,8},{10,9},{11,1... | collective-permute-start | bytes 824 | tf_op jit(solution)/shard_map/ppermute | solution.py:18
  34.3 0.7 %slice-start = ((f32[2,1,256]{2,1,0:T(1,128)}), f32[1,1,256]{2,1,0:T(1,128)S(1)}, s32[]{:S(2)}) async-start(f32[2,1,256]{2,1,0:T(1,128)} %copy-done.5), calls=%async_computation.2 | async-start | bytes 2048 | tf_op jit(solution)/shard_map/slice | solution.py:78
  35.0 1.3 %copy-start.6 = (f32[2,1,256]{2,1,0:T(1,128)S(1)}, f32[2,1,256]{2,1,0:T(1,128)}, u32[]{:S(2)}) copy-start(f32[2,1,256]{2,1,0:T(1,128)} %copy-done.5) | copy-start | bytes 6148
